TPU v7x, 128 devices: a whole 4x4x4 slice. The times are simulated.
128 devices in a mesh: dp: 2 (over core), ep: 64 (over z, y, x).
Axes of the slice: x: 4, y: 4, z: 4, core: 2. Of those that a mesh axis runs over, the one named last changes fastest.
Arguments:
- x_tokens: bfloat16 [65536, 768], P(('dp', 'ep'))
- expert_id: int32 [65536], P(('dp', 'ep'))
- token_slot: int32 [65536], P(('dp', 'ep'))
- grad_y: bfloat16 [65536, 768], P(('dp', 'ep'))
- w_router: float32 [768, 64], replicated
- w_in: bfloat16 [64, 768, 3072], P('ep')
- w_out: bfloat16 [64, 3072, 768], P('ep')
- row_in: float32 [64, 768], P('ep')
- col_in: float32 [64, 3072], P('ep')
- row_out: float32 [64, 3072], P('ep')
- col_out: float32 [64, 768], P('ep')
- row_router: float32 [768], replicated
- col_router: float32 [64], replicated
Outputs:
- output 1: bfloat16 [64, 768, 3072], P('ep')
- output 2: bfloat16 [64, 3072, 768], P('ep')
- output 3: float32 [768, 64], replicated
- output 4: float32 [64, 768], P('ep')
- output 5: float32 [64, 3072], P('ep')
- output 6: float32 [64, 3072], P('ep')
- output 7: float32 [64, 768], P('ep')
- output 8: float32 [768], replicated
- output 9: float32 [64], replicated
- output 10: bfloat16 [65536, 768], P(('dp', 'ep'))
All inputs are finite; a program needn't handle non-finite values.
Results may differ from a plain program's by a relative error of at most 0.00445.
Values are sent between devices in bfloat16 or wider.
A program may use at most 1 GiB of HBM per device.

v0:
```python
import jax
import jax.numpy as jnp
from jax import lax
from jax.sharding import PartitionSpec as P
import math

OPT_STEP = 2
DECAY_RATE = 1.0 - OPT_STEP ** -0.8
LR_BASE = min(0.01, 1.0 / math.sqrt(OPT_STEP))
AUX_COEF = 0.01
PRECISE = lax.Precision.HIGHEST


def optimizer_step(weight, gradient, row_stat, col_stat):
    grad_sq = gradient * gradient + 1e-30
    row_new = DECAY_RATE * row_stat + (1.0 - DECAY_RATE) * jnp.mean(grad_sq, axis=-1)
    col_new = DECAY_RATE * col_stat + (1.0 - DECAY_RATE) * jnp.mean(grad_sq, axis=-2)
    row_norm = row_new / jnp.mean(row_new, axis=-1, keepdims=True)
    update = gradient * lax.rsqrt(row_norm)[..., :, None] * lax.rsqrt(col_new)[..., None, :]
    upd_rms = jnp.sqrt(jnp.mean(update * update, axis=(-2, -1), keepdims=True))
    update = update / jnp.maximum(1.0, upd_rms)
    w_full = weight.astype(jnp.float32)
    w_rms = jnp.sqrt(jnp.mean(w_full * w_full, axis=(-2, -1), keepdims=True))
    new_weight = w_full - LR_BASE * jnp.maximum(1e-3, w_rms) * update
    return new_weight, row_new, col_new


def solution(mesh):
    ep_size = mesh.shape['ep']
    tok_spec = P(('dp', 'ep'))
    row_spec = P(('dp', 'ep'), None)
    exp_spec = P('ep')
    full_spec = P()

    def local_step(x_tokens, expert_id, token_slot, grad_y, w_router, w_in, w_out, row_in, col_in, row_out, col_out, row_router, col_router):
        tokens, width = x_tokens.shape
        experts_local = w_in.shape[0]
        experts = w_router.shape[1]
        capacity = 5 * tokens // (4 * experts)
        x_wide = x_tokens.astype(jnp.float32)
        logits = jnp.dot(x_wide, w_router, precision=PRECISE)
        gate_probs = jax.nn.softmax(logits, axis=-1)
        onehot = (expert_id[:, None] == jnp.arange(experts)[None, :]).astype(jnp.float32)
        gate_val = jnp.sum(gate_probs * onehot, axis=-1)
        flat_pos = jnp.where(token_slot >= 0, expert_id * capacity + token_slot, experts * capacity)
        src_tok = jnp.full((experts * capacity,), tokens, jnp.int32).at[flat_pos].set(jnp.arange(tokens, dtype=jnp.int32), mode='drop')

        def to_experts(token_rows):
            send_buf = jnp.take(token_rows, src_tok, axis=0, mode='fill', fill_value=0)
            send_buf = send_buf.reshape(ep_size, experts_local, capacity, width)
            recv_buf = lax.all_to_all(send_buf, 'ep', 0, 2, tiled=True)
            return recv_buf.reshape(experts_local, ep_size * capacity, width)

        def to_tokens(expert_rows):
            back_buf = lax.all_to_all(expert_rows.reshape(1, experts_local, ep_size * capacity, width), 'ep', 2, 0, tiled=True)
            back_buf = back_buf.reshape(experts * capacity, width)
            return jnp.take(back_buf, flat_pos, axis=0, mode='fill', fill_value=0)

        recv_x = to_experts(x_tokens)
        pre_act = jnp.einsum('erd,edf->erf', recv_x, w_in, preferred_element_type=jnp.float32).astype(jnp.bfloat16)
        hid_act = jnp.maximum(pre_act, 0)
        exp_out = jnp.einsum('erf,efd->erd', hid_act, w_out, preferred_element_type=jnp.float32).astype(jnp.bfloat16)
        out_tok = to_tokens(exp_out)
        grad_gate = jnp.einsum('td,td->t', grad_y, out_tok, preferred_element_type=jnp.float32)
        grad_h = (gate_val[:, None] * grad_y).astype(jnp.bfloat16)
        recv_gh = to_experts(grad_h)
        grad_act = jnp.einsum('erd,efd->erf', recv_gh, w_out, preferred_element_type=jnp.float32)
        grad_pre = jnp.where(pre_act > 0, grad_act, 0.0).astype(jnp.bfloat16)
        grad_wout = jnp.einsum('erf,erd->efd', hid_act, recv_gh, preferred_element_type=jnp.float32)
        grad_win = jnp.einsum('erd,erf->edf', recv_x, grad_pre, preferred_element_type=jnp.float32)
        grad_buf = jnp.einsum('erf,edf->erd', grad_pre, w_in, preferred_element_type=jnp.float32).astype(jnp.bfloat16)
        dx_expert = to_tokens(grad_buf)
        grad_win = lax.psum(grad_win, 'dp')
        grad_wout = lax.psum(grad_wout, 'dp')
        route_frac = jnp.mean(onehot, axis=0)
        grad_prob = onehot * grad_gate[:, None] + AUX_COEF * experts * route_frac[None, :] / tokens
        grad_logits = gate_probs * (grad_prob - jnp.sum(gate_probs * grad_prob, axis=-1, keepdims=True))
        grad_router = lax.psum(jnp.einsum('td,te->de', x_wide, grad_logits, precision=PRECISE), ('dp', 'ep'))
        grad_x = (dx_expert.astype(jnp.float32) + jnp.einsum('te,de->td', grad_logits, w_router, precision=PRECISE)).astype(jnp.bfloat16)
        new_in, row_in_new, col_in_new = optimizer_step(w_in, grad_win, row_in, col_in)
        new_out, row_out_new, col_out_new = optimizer_step(w_out, grad_wout, row_out, col_out)
        new_router, row_router_new, col_router_new = optimizer_step(w_router, grad_router, row_router, col_router)
        return (new_in.astype(jnp.bfloat16), new_out.astype(jnp.bfloat16), new_router, row_in_new, col_in_new, row_out_new, col_out_new, row_router_new, col_router_new, grad_x)

    in_specs = (row_spec, tok_spec, tok_spec, row_spec, full_spec, exp_spec, exp_spec, exp_spec, exp_spec, exp_spec, exp_spec, full_spec, full_spec)
    out_specs = (exp_spec, exp_spec, full_spec, exp_spec, exp_spec, exp_spec, exp_spec, full_spec, full_spec, row_spec)
    return jax.shard_map(local_step, mesh=mesh, in_specs=in_specs, out_specs=out_specs, check_vma=False)
```

profile of v0, /device:TPU:1, one launch (start us, length us, event | category | flops | bytes accessed | tf_op | source)
XLA Modules:
  0.0 389.4 jit_solution(4562953741247235460)
XLA Ops:
  14.5 38.7 %all_to_all.16 = bf16[64,1,10,768]{3,2,1,0:T(8,128)(2,1)} all-to-all(bf16[64,1,10,768]{3,2,1,0:T(8,128)(2,1)S(1)} %bitcast.70), channel_id=1, replica_groups=mesh['dp'=2,'ep'=64] {'ep'}, dimensions={0} | all-to-all | bytes 1966080 | tf_op jit(solution)/shard_map/all_to_all | solution.py:51
  55.5 6.2 %convolution_convert_fusion = bf16[640,3072]{1,0:T(8,128)(2,1)S(1)} fusion(bf16[640,768]{1,0:T(8,128)(2,1)S(1)} %reshape.254, bf16[1,768,3072]{2,1,0:T(8,128)(2,1)} %param.22), kind=kOutput, calls=%fused_computation.26 | convolution fusion | flops 3021864960 | bytes 9633792 | tf_op jit(solution)/shard_map/erd,edf->erf/dot_general | solution.py:60
  67.0 7.6 %reduce.16 = bf16[640,768]{1,0:T(8,128)(2,1)} reduce(bf16[640,1,1,768]{3,2,1,0:T(2,128)(2,1)S(1)} %bitcast.65, bf16[]{:T(256)} %broadcast.171), dimensions={1,2}, to_apply=%bitcast.57.reduce_sub_computation | reduce | bytes 1966082
  74.6 3.6 reshape.323
  78.3 4.6 %all-to-all-start.2 = ((bf16[64,2,3840]{2,1,0:T(2,128)(2,1)}), bf16[64,2,3840]{2,1,0:T(2,128)(2,1)S(1)}, u32[]{:S(2)}, u32[]{:S(2)}) async-start(bf16[64,2,3840]{2,1,0:T(2,128)(2,1)} %reshape.323), calls=%async_computation.2 | async-start | bytes 1966080 | tf_op jit(solution)/shard_map/all_to_all | solution.py:55
  85.1 13.5 %all-to-all-done.2 = bf16[64,2,3840]{2,1,0:T(2,128)(2,1)S(1)} async-done(((bf16[64,2,3840]{2,1,0:T(2,128)(2,1)}), bf16[64,2,3840]{2,1,0:T(2,128)(2,1)S(1)}, u32[]{:S(2)}, u32[]{:S(2)}) %all-to-all-start.2) | async-done | bytes 983072 | tf_op jit(solution)/shard_map/all_to_all | solution.py:55
  112.5 7.5 %all-to-all-start.1 = ((bf16[64,1,10,768]{3,2,1,0:T(8,128)(2,1)}), bf16[64,1,10,768]{3,2,1,0:T(8,128)(2,1)S(1)}, u32[]{:S(2)}, u32[]{:S(2)}) async-start(bf16[64,1,10,768]{3,2,1,0:T(8,128)(2,1)} %bitcast.69), calls=%async_computation.1 | async-start | bytes 3145728 | tf_op jit(solution)/shard_map/all_to_all | solution.py:51
  121.4 24.9 %all-to-all-done.1 = bf16[64,1,10,768]{3,2,1,0:T(8,128)(2,1)S(1)} async-done(((bf16[64,1,10,768]{3,2,1,0:T(8,128)(2,1)}), bf16[64,1,10,768]{3,2,1,0:T(8,128)(2,1)S(1)}, u32[]{:S(2)}, u32[]{:S(2)}) %all-to-all-start.1) | async-done | bytes 983072 | tf_op jit(solution)/shard_map/all_to_all | solution.py:51
  147.4 7.2 %select_convert_fusion = bf16[640,3072]{1,0:T(8,128)(2,1)S(1)} fusion(bf16[640,3072]{1,0:T(8,128)(2,1)} %copy-done.29, bf16[640,768]{1,0:T(8,128)(2,1)} %reshape.257, bf16[1,3072,768]{2,1,0:T(8,128)(2,1)} %param.23), kind=kOutput, calls=%fused_computation.23 | convolution fusion | flops 3025797120 | bytes 13565952 | tf_op jit(solution)/shard_map/erd,efd->erf/dot_general | solution.py:67
  154.7 6.3 %convolution_bitcast_fusion = f32[1,3072,768]{2,1,0:T(8,128)} fusion(bf16[640,768]{1,0:T(8,128)(2,1)S(1)} %copy-done.11, bf16[640,3072]{1,0:T(8,128)(2,1)S(1)} %copy-done.30), kind=kOutput, calls=%fused_computation.24 | convolution fusion | flops 3021864960 | bytes 14352384 | tf_op jit(solution)/shard_map/erf,erd->efd/dot_general | solution.py:69
  161.0 6.4 %convolution_bitcast_fusion.1 = f32[1,768,3072]{2,1,0:T(8,128)} fusion(bf16[640,768]{1,0:T(8,128)(2,1)S(1)} %copy-done.5, bf16[640,3072]{1,0:T(8,128)(2,1)S(1)} %select_convert_fusion), kind=kOutput, calls=%fused_computation.25 | convolution fusion | flops 3019898880 | bytes 14352384 | tf_op jit(solution)/shard_map/erd,erf->edf/dot_general | solution.py:70
  167.5 5.4 %fusion.2 = f32[]{:T(128)} fusion(bf16[1,3072,768]{2,1,0:T(8,128)(2,1)} %param.23), kind=kLoop, calls=%fused_computation.11 | loop fusion | flops 7077887 | bytes 4718596 | tf_op jit(solution)/shard_map/reduce_sum | solution.py:23
  173.6 5.4 %fusion = f32[]{:T(128)} fusion(bf16[1,768,3072]{2,1,0:T(8,128)(2,1)} %param.22), kind=kLoop, calls=%fused_computation.9 | loop fusion | flops 7077887 | bytes 4718596 | tf_op jit(solution)/shard_map/reduce_sum | solution.py:23
  181.0 94.4 %all-reduce.4.cloned.1.call-done = f32[768,64]{0,1:T(8,128)} async-done(((f32[768,64]{0,1:T(8,128)}), f32[768,64]{0,1:T(8,128)}) %all-reduce.4.cloned.1.call-update) | async-done | bytes 196624 | tf_op jit(solution)/shard_map/psum | solution.py:78
  276.5 6.8 %fusion.33 = bf16[1,1,640,768]{3,2,1,0:T(8,128)(2,1)S(1)} fusion(bf16[640,3072]{1,0:T(8,128)(2,1)} %copy-done.3, bf16[1,768,3072]{2,1,0:T(8,128)(2,1)} %param.22), kind=kOutput, calls=%fused_computation.45 | convolution fusion | flops 3020390400 | bytes 9633792 | tf_op jit(solution)/shard_map/erf,edf->erd/dot_general | solution.py:71
  284.8 7.6 %reduce.17 = bf16[640,768]{1,0:T(8,128)(2,1)} reduce(bf16[640,1,1,768]{3,2,1,0:T(2,128)(2,1)S(1)} %bitcast.66, bf16[]{:T(256)} %broadcast.171), dimensions={1,2}, to_apply=%bitcast.56.reduce_sub_computation | reduce | bytes 1966082
  295.7 7.7 %all-to-all-start.3 = ((bf16[64,2,3840]{2,1,0:T(2,128)(2,1)}), bf16[64,2,3840]{2,1,0:T(2,128)(2,1)S(1)}, u32[]{:S(2)}, u32[]{:S(2)}) async-start(bf16[64,2,3840]{2,1,0:T(2,128)(2,1)} %reshape.325), calls=%async_computation.3 | async-start | bytes 1966080 | tf_op jit(solution)/shard_map/all_to_all | solution.py:55
  307.4 14.3 %all-to-all-done.3 = bf16[64,2,3840]{2,1,0:T(2,128)(2,1)S(1)} async-done(((bf16[64,2,3840]{2,1,0:T(2,128)(2,1)}), bf16[64,2,3840]{2,1,0:T(2,128)(2,1)S(1)}, u32[]{:S(2)}, u32[]{:S(2)}) %all-to-all-start.3) | async-done | bytes 983072 | tf_op jit(solution)/shard_map/all_to_all | solution.py:55
  331.1 8.3 %all-reduce.6.cloned.1.call-done = (f32[1,768,3072]{2,1,0:T(8,128)}, f32[1,3072,768]{2,1,0:T(8,128)}) async-done(((f32[1,768,3072]{2,1,0:T(8,128)}, f32[1,3072,768]{2,1,0:T(8,128)}), (f32[1,768,3072]{2,1,0:T(8,128)}, f32[1,3072,768]{2,1,0:T(8,128)})) %all-reduce.6.cloned.1.call-update) | async-done | bytes 18874384 | tf_op jit(solution)/shard_map/psum | solution.py:73
  339.4 5.5 %fusion.5 = (f32[768]{0:T(1024)S(1)}, f32[3072]{0:T(1024)S(1)}) fusion(f32[1,768,3072]{2,1,0:T(8,128)} %get-tuple-element.20), kind=kLoop, calls=%fused_computation.20 | loop fusion | flops 9433344 | bytes 9452544 | tf_op jit(solution)/shard_map/reduce_sum | solution.py:16
  350.5 6.8 %multiply_reduce_fusion.1 = f32[]{:T(128)} fusion(f32[1,768,3072]{2,1,0:T(8,128)} %get-tuple-element.20, f32[3072]{0:T(1024)S(1)} %bitcast.73, f32[768]{0:T(1024)S(1)} %rsqrt_reduce_fusion.1), kind=kLoop, calls=%fused_computation.16 | loop fusion | flops 9437183 | bytes 9452548 | tf_op jit(solution)/shard_map/reduce_sum | solution.py:20
  358.7 6.4 %multiply_reduce_fusion = f32[]{:T(128)} fusion(f32[1,3072,768]{2,1,0:T(8,128)} %get-tuple-element.21, f32[768]{0:T(1024)S(1)} %get-tuple-element.28, f32[3072]{0:T(1024)S(1)} %bitcast.71), kind=kLoop, calls=%fused_computation.13 | loop fusion | flops 9437183 | bytes 9452548 | tf_op jit(solution)/shard_map/reduce_sum | solution.py:20
  365.8 8.9 %fusion.1 = bf16[1,768,3072]{2,1,0:T(8,128)(2,1)} fusion(bf16[1,768,3072]{2,1,0:T(8,128)(2,1)} %param.22, f32[1,768,3072]{2,1,0:T(8,128)} %get-tuple-element.20, f32[]{:T(128)S(6)} %max.31, f32[3072]{0:T(1024)S(1)} %bitcast.74, f32[768]{0:T(1024)S(1)} %rsqrt_reduce_fusion.1, f32[]{:T(128)S(6)} %mul.251), kind=kLoop, calls=%fused_computation.10 | loop fusion | flops 16515072 | bytes 18889736 | tf_op jit(solution)/shard_map/convert_element_type | solution.py:83
  374.7 7.7 %fusion.3 = bf16[1,3072,768]{2,1,0:T(8,128)(2,1)} fusion(bf16[1,3072,768]{2,1,0:T(8,128)(2,1)S(1)} %bitcast.64, f32[1,3072,768]{2,1,0:T(8,128)} %get-tuple-element.21, f32[]{:T(128)S(6)} %max.34, f32[768]{0:T(1024)S(1)} %get-tuple-element.28, f32[3072]{0:T(1024)S(1)} %bitcast.72, f32[]{:T(128)S(6)} %mul.276), kind=kLoop, calls=%fused_computation.12 | loop fusion | flops 16515072 | bytes 18889736 | tf_op jit(solution)/shard_map/convert_element_type | solution.py:83
  (127 shorter events, 56.7 us)
Async XLA Ops:
  53.2 8.5 %slice-start = ((s8[4718592]{0:T(1024)(128)(4,1)}), s8[524288]{0:T(1024)(128)(4,1)S(1)}, s32[]{:S(2)}) async-start(s8[4718592]{0:T(1024)(128)(4,1)} %bitcast.61), calls=%async_computation.6 | async-start | bytes 1048576
  65.0 18.0 %copy-start.13 = (s32[512]{0:T(512)S(1)}, s32[512]{0:T(512)}, u32[]{:S(2)}) copy-start(s32[512]{0:T(512)} %param.18) | copy-start | bytes 6148
  65.0 18.1 %copy-start.8 = (f32[768,64]{0,1:T(8,128)S(1)}, f32[768,64]{0,1:T(8,128)}, u32[]{:S(2)}) copy-start(f32[768,64]{0,1:T(8,128)} %param.21) | copy-start | bytes 589828
  78.3 20.3 %all-to-all-start.2 = ((bf16[64,2,3840]{2,1,0:T(2,128)(2,1)}), bf16[64,2,3840]{2,1,0:T(2,128)(2,1)S(1)}, u32[]{:S(2)}, u32[]{:S(2)}) async-start(bf16[64,2,3840]{2,1,0:T(2,128)(2,1)} %reshape.323), calls=%async_computation.2 | async-start | bytes 1966080 | tf_op jit(solution)/shard_map/all_to_all | solution.py:55
  83.9 17.9 %copy-start.9 = (f32[512,64]{0,1:T(8,128)}, f32[512,64]{0,1:T(8,128)S(1)}, u32[]{:S(2)}) copy-start(f32[512,64]{0,1:T(8,128)S(1)} %get-tuple-element.37) | copy-start | bytes 393220
  111.0 9.1 %copy-start.10 = (f32[512,64]{0,1:T(8,128)S(1)}, f32[512,64]{0,1:T(8,128)}, u32[]{:S(2)}) copy-start(f32[512,64]{0,1:T(8,128)} %copy-done.9) | copy-start | bytes 393220
  111.0 9.1 %copy-start.20 = (f32[512]{0:T(512)S(1)}, f32[512]{0:T(512)}, u32[]{:S(2)}) copy-start(f32[512]{0:T(512)} %fusion.39) | copy-start | bytes 6148
  111.0 9.1 %copy-start.22 = (f32[512]{0:T(512)S(1)}, f32[512]{0:T(512)}, u32[]{:S(2)}) copy-start(f32[512]{0:T(512)} %copy-done.21) | copy-start | bytes 6148
  111.0 9.1 %copy-start.27 = (f32[64]{0:T(128)S(1)}, f32[64]{0:T(128)}, u32[]{:S(2)}) copy-start(f32[64]{0:T(128)} %broadcast_multiply_fusion.4) | copy-start | bytes 772
  112.5 33.8 %all-to-all-start.1 = ((bf16[64,1,10,768]{3,2,1,0:T(8,128)(2,1)}), bf16[64,1,10,768]{3,2,1,0:T(8,128)(2,1)S(1)}, u32[]{:S(2)}, u32[]{:S(2)}) async-start(bf16[64,1,10,768]{3,2,1,0:T(8,128)(2,1)} %bitcast.69), calls=%async_computation.1 | async-start | bytes 3145728 | tf_op jit(solution)/shard_map/all_to_all | solution.py:51
  120.0 155.4 %all-reduce.4.cloned.1.call-start = ((), (), s32[]{:S(2)}) async-start(), calls=%async_computation.4 | async-start | bytes 393216 | tf_op jit(solution)/shard_map/psum | solution.py:78
  121.4 218.0 %all-reduce.6.cloned.1.call-start = ((), (), s32[]{:S(2)}) async-start(), calls=%async_computation.5 | async-start | bytes 37748736 | tf_op jit(solution)/shard_map/psum | solution.py:73
  147.4 7.2 %copy-start.11 = (bf16[640,768]{1,0:T(8,128)(2,1)S(1)}, bf16[640,768]{1,0:T(8,128)(2,1)}, u32[]{:S(2)}) copy-start(bf16[640,768]{1,0:T(8,128)(2,1)} %reshape.257) | copy-start | bytes 2949124
  147.4 7.2 %copy-start.30 = (bf16[640,3072]{1,0:T(8,128)(2,1)S(1)}, bf16[640,3072]{1,0:T(8,128)(2,1)}, u32[]{:S(2)}) copy-start(bf16[640,3072]{1,0:T(8,128)(2,1)} %copy-done.29) | copy-start | bytes 11796484
  283.3 20.1 %copy-start.23 = (f32[768]{0:T(1024)S(1)}, f32[768]{0:T(1024)}, u32[]{:S(2)}) copy-start(f32[768]{0:T(1024)} %param.28) | copy-start | bytes 9220
  283.3 21.4 %copy-start.28 = (f32[64]{0:T(128)S(1)}, f32[64]{0:T(128)}, u32[]{:S(2)}) copy-start(f32[64]{0:T(128)} %param.29) | copy-start | bytes 772
  283.3 21.9 %copy-start.7 = (f32[768,64]{0,1:T(8,128)S(1)}, f32[768,64]{0,1:T(8,128)}, u32[]{:S(2)}) copy-start(f32[768,64]{0,1:T(8,128)} %all-reduce.4.cloned.1.call-done) | copy-start | bytes 589828
  295.7 26.0 %all-to-all-start.3 = ((bf16[64,2,3840]{2,1,0:T(2,128)(2,1)}), bf16[64,2,3840]{2,1,0:T(2,128)(2,1)S(1)}, u32[]{:S(2)}, u32[]{:S(2)}) async-start(bf16[64,2,3840]{2,1,0:T(2,128)(2,1)} %reshape.325), calls=%async_computation.3 | async-start | bytes 1966080 | tf_op jit(solution)/shard_map/all_to_all | solution.py:55
  304.0 24.7 %copy-start.14 = (f32[768]{0:T(1024)}, f32[768]{0:T(1024)S(1)}, u32[]{:S(2)}) copy-start(f32[768]{0:T(1024)S(1)} %get-tuple-element.23) | copy-start | bytes 9220
  348.6 8.7 %copy-start.15 = (f32[1,768]{1,0:T(1,128)}, f32[1,768]{1,0:T(1,128)S(1)}, u32[]{:S(2)}) copy-start(f32[1,768]{1,0:T(1,128)S(1)} %get-tuple-element.39) | copy-start | bytes 9220
  350.5 8.1 %copy-start.12 = (f32[1,3072]{1,0:T(1,128)}, f32[1,3072]{1,0:T(1,128)S(1)}, u32[]{:S(2)}) copy-start(f32[1,3072]{1,0:T(1,128)S(1)} %get-tuple-element.27) | copy-start | bytes 36868
  358.7 16.0 %slice-start.2 = ((s8[4718592]{0:T(1024)(128)(4,1)}), s8[524288]{0:T(1024)(128)(4,1)S(1)}, s32[]{:S(2)}) async-start(s8[4718592]{0:T(1024)(128)(4,1)} %bitcast.63), calls=%async_computation.8 | async-start | bytes 1048576
  365.8 8.9 %slice-start.3 = ((s8[4718592]{0:T(1024)(128)(4,1)}), s8[4194304]{0:T(1024)(128)(4,1)S(1)}, s32[]{:S(2)}) async-start(s8[4718592]{0:T(1024)(128)(4,1)} %bitcast.63), calls=%async_computation.9 | async-start | bytes 8388608
  374.7 7.7 %copy-start.1 = (bf16[512,768]{1,0:T(8,128)(2,1)S(1)}, bf16[512,768]{1,0:T(8,128)(2,1)}, u32[]{:S(2)}) copy-start(bf16[512,768]{1,0:T(8,128)(2,1)} %param.17) | copy-start | bytes 2359300
  (16 other events, 63.5 us)
Sparse Core Ops, SparseCore 0:
  126.1 149.2 all-reduce.3
  278.1 61.2 all-reduce.5
where the time goes:
time: 393 us; the launch traced here: 389 us
  waiting for transfers between devices  155 us (39%)
  other arithmetic  74.8 us (19%)
  matrix products  40.7 us (10%)
  local copies, waits for them, and re-layouts  38.9 us (10%)
  blocking collectives  38.7 us (10%)
  between operations  21.1 us (5%)
  starting transfers between devices  20 us (5%)
    psum x1, waiting for transfers between devices, local_step(): lax.psum(jnp.einsum('td,te->de', x_wide, grad_logits, precision=PRECISE),...  94.4 us
    all_to_all x1, blocking collectives, to_experts(): recv_buf = lax.all_to_all(send_buf, 'ep', 0, 2, tiled=True)  38.7 us
    all_to_all x2, waiting for transfers between devices, to_tokens(): lax.all_to_all(expert_rows.reshape(1, experts_local, ep_size * capacity,...  27.8 us
    all_to_all x1, waiting for transfers between devices, to_experts(): recv_buf = lax.all_to_all(send_buf, 'ep', 0, 2, tiled=True)  24.9 us
    unnamed x77, local copies, waits for them, and re-layouts  18.4 us
    unnamed x4, other arithmetic  15.2 us
    reduce_sum x3, other arithmetic, optimizer_step(): upd_rms = jnp.sqrt(jnp.mean(update * update, axis=(-2, -1), keepdims=True))  13.9 us
    all_to_all x2, starting transfers between devices, to_tokens(): lax.all_to_all(expert_rows.reshape(1, experts_local, ep_size * capacity,...  12.4 us
  transfers between devices with their start and end apart: 5, of which 5 were waited for; matrix products, arithmetic and copies ran while one was open for 17% of the time, Pallas kernels for 0%

commit v1 on v0

v1 whole, which is shorter than its diff:
```python
import functools
import math

import jax
import jax.numpy as jnp
from jax import lax
from jax.experimental import pallas as pl
from jax.experimental.pallas import tpu as pltpu
from jax.sharding import PartitionSpec as P

OPT_STEP = 2
DECAY = 1.0 - OPT_STEP ** -0.8
LR = min(0.01, 1.0 / math.sqrt(OPT_STEP))
AUX = 0.01
MESH = pl.DeviceIdType.MESH
VMEM = pltpu.VMEM
bf16 = jnp.bfloat16
f32 = jnp.float32

N = 64
T = 512
D = 768
F = 3072
H = F // 2
C = 10
R = N * C
J = C // 2
L = 128
FT = 512
DT = 256
BLOCKS = ((0, 3), (3, J))


def dot(a, b, ca, cb):
    return lax.dot_general(a, b, (((ca,), (cb,)), ((), ())), preferred_element_type=f32)


def split3(v):
    hi = v.astype(bf16)
    rest = v - hi.astype(f32)
    mid = rest.astype(bf16)
    return hi, mid, (rest - mid.astype(f32)).astype(bf16)


def probs(logits3):
    logits = (logits3[:, 2 * L:] + logits3[:, L:2 * L]) + logits3[:, :L]
    lane = lax.broadcasted_iota(jnp.int32, logits.shape, 1)
    logits = jnp.where(lane < N, logits, -jnp.inf)
    e = jnp.exp(logits - jnp.max(logits, axis=1, keepdims=True))
    return e / jnp.sum(e, axis=1, keepdims=True)


def tr(v):
    return jnp.swapaxes(v, 0, 1)


def mean1(v):
    return jnp.sum(v, axis=1, keepdims=True) * (1.0 / v.shape[1])


def total(v):
    return jnp.sum(jnp.sum(v, axis=0, keepdims=True), axis=1, keepdims=True)


def kernel(x_hbm, dy_hbm, eid_ref, slot_ref, wrt_ref, win_hbm, wout_hbm,
           rin_ref, cin_ref, rout_ref, cout_ref, rr_ref, cr_ref,
           win_new, wout_new, wrt_new, rin_new, cin_new, rout_new, cout_new, rr_new, cr_new, dx_ref,
           win, wout, xv, dyv, sx, sdy, rx, rdy, xb, dyb, hb, dhb, act, da, gout, gin,
           wr3, p_tok, oh_tok, t_oh, pe_scr, gs, gr, rs_s, rs_r, ag_s, ag_r, back,
           st_s, st_r, hs_s, hs_r, sem_l,
           xs_s, xs_r, ds_s, ds_r, gs_s, gs_r, bs_s, bs_r, rss, rsr, ags, agr, dps, dpr):
    me = lax.axis_index("ep")
    c = lax.axis_index("dp")
    oc = 1 - c
    my_h = pl.multiple_of(c * H, H)
    ot_h = pl.multiple_of(oc * H, H)
    halves = (ot_h, my_h)
    barrier = pltpu.get_barrier_semaphore()
    z, y, x = me // 16, (me // 4) % 4, me % 4
    along_x = [(x + k) % 4 for k in range(4)]

    def peers(act_on):
        for k in range(1, 4):
            act_on(z * 16 + y * 4 + along_x[k])

        def step(n, _):
            base = ((z + n // 4) % 4) * 16 + ((y + n % 4) % 4) * 4
            for k in range(4):
                act_on(base + along_x[k])
            return 0
        lax.fori_loop(1, 16, step, 0)

    peers(lambda p: pl.semaphore_signal(barrier, inc=1, device_id={"ep": p}, device_id_type=MESH))
    pl.semaphore_signal(barrier, inc=1, device_id={"dp": oc}, device_id_type=MESH)

    loads = [pltpu.make_async_copy(src, dst, sem_l.at[n]) for n, (src, dst) in enumerate(
        ((x_hbm, xv), (dy_hbm, dyv), (win_hbm.at[0], win), (wout_hbm.at[0], wout)))]
    for load in loads:
        load.start()

    def send_all(src, dst, s, r):
        def go(p):
            pltpu.make_async_remote_copy(src(p), dst(me), s, r, device_id={"ep": p}, device_id_type=MESH).start()
        peers(go)

    def done_all(src, dst, s, r):
        most = pl.ds(0, N - 1)
        return pltpu.make_async_remote_copy(src(most), dst(most), s, r, device_id={"ep": me}, device_id_type=MESH)

    def swap(src, dst, n):
        return pltpu.make_async_remote_copy(src, dst, dps.at[n], dpr.at[n], device_id={"dp": oc}, device_id_type=MESH)

    def lanes_of(ref, b):
        lo, hi = BLOCKS[b]
        return lambda p: ref.at[p, :, lo * D:hi * D]

    def rows_of(ref):
        return lambda p: ref.at[p]

    x_io = (rows_of(sx), rows_of(rx), xs_s, xs_r)
    dy_io = [(lanes_of(sdy, b), lanes_of(rdy, b), ds_s.at[b], ds_r.at[b]) for b in range(2)]
    bk_io = [(lanes_of(sx, b), lanes_of(back, b), bs_s.at[b], bs_r.at[b]) for b in range(2)]
    g_io = (rows_of(gs), rows_of(gr), gs_s, gs_r)
    rs_io = (rows_of(rs_s), rows_of(rs_r), rss, rsr)

    eid = eid_ref[...]
    slot = slot_ref[...]
    code = jnp.where(slot >= 0, (slot >> 1) * L + 2 * eid + (slot & 1), -1)

    def dispatch(rows_ref, out_ref):
        rows = rows_ref[...]
        for j in range(J):
            pick = (lax.broadcasted_iota(jnp.int32, (L, T), 0) + j * L == code).astype(f32).astype(bf16)
            out_ref[:, :, j * D:(j + 1) * D] = dot(pick, rows, 1, 0).astype(bf16).reshape(N, 2, D)

    loads[0].wait()
    dispatch(xv, sx)
    pl.semaphore_wait(barrier, N)
    send_all(*x_io)
    loads[1].wait()
    dispatch(dyv, sdy)
    wrt = wrt_ref[...]
    for n, part in enumerate(split3(wrt)):
        wr3[n * L:(n + 1) * L, :] = jnp.concatenate([part, jnp.zeros_like(part)], axis=0)
    p_tok[...] = probs(dot(xv[...], wr3[...], 1, 1))
    e_col = tr(jnp.broadcast_to(eid.astype(f32), (L, T)))
    code_col = tr(jnp.broadcast_to(code.astype(f32), (L, T)))
    lane_t = lax.broadcasted_iota(jnp.int32, (T, L), 1)
    oh_tok[...] = (lane_t.astype(f32) == e_col).astype(f32)
    for j in range(J):
        t_oh[:, j * L:(j + 1) * L] = (lane_t + j * L == code_col.astype(jnp.int32)).astype(f32).astype(bf16)

    def sum_sq(ref, rows):
        def step(n, acc):
            v = ref[pl.ds(pl.multiple_of(n * 32, 32), 32), :].astype(f32)
            return acc + v * v
        return total(lax.fori_loop(0, rows // 32, step, jnp.zeros((32, ref.shape[1]), f32)))

    loads[2].wait()
    win_rms = jnp.sqrt(sum_sq(win, D) * (1.0 / (D * F)))
    done_all(*x_io).wait_send()
    send_all(*dy_io[0])
    loads[3].wait()
    wout_rms = jnp.sqrt(sum_sq(wout, F) * (1.0 / (D * F)))
    wr_rms = jnp.sqrt(total(wrt * wrt) * (1.0 / (D * N)))

    done_all(*x_io).wait_recv()
    rx[pl.ds(me, 1)] = sx[pl.ds(me, 1)]
    for j in range(J):
        xb[0, j * L:(j + 1) * L, :] = rx[:, :, j * D:(j + 1) * D].reshape(L, D)
    sw_x = swap(xb.at[0], xb.at[1], 0)
    sw_x.start()
    for s in range(2):
        for n in range(H // FT):
            a = dot(xb[0], win[:, pl.ds(halves[s] + n * FT, FT)], 1, 0).astype(bf16)
            act[s, :, n * FT:(n + 1) * FT] = jnp.maximum(a, 0)
        if s == 0:
            sw_act = swap(act.at[0], act.at[2], 1)
            sw_act.start()
    done_all(*dy_io[0]).wait_send()
    send_all(*dy_io[1])
    pe = probs(dot(xb[0], wr3[...], 1, 1))
    lane_r = lax.broadcasted_iota(jnp.int32, (R, L), 1)
    pe_scr[...] = jnp.broadcast_to(jnp.sum(jnp.where(lane_r == me, pe, 0.0), axis=1, keepdims=True), (R, L))
    for n in range(D // DT):
        cols = slice(n * DT, (n + 1) * DT)
        h = dot(act[0], wout[pl.ds(ot_h, H), cols], 1, 0) + dot(act[1], wout[pl.ds(my_h, H), cols], 1, 0)
        hb[:, cols] = h.astype(bf16)

    lane = lax.broadcasted_iota(jnp.int32, (L, L), 1)
    odd = lax.broadcasted_iota(jnp.int32, (L, L), 0) & 1
    wide = jnp.zeros((L, L), f32)
    sw_dh, sw_da = [], []
    for b, (lo, hi) in enumerate(BLOCKS):
        rows = slice(lo * L, hi * L)
        done_all(*dy_io[b]).wait_recv()
        rdy[pl.ds(me, 1), :, lo * D:hi * D] = sdy[pl.ds(me, 1), :, lo * D:hi * D]
        for j in range(lo, hi):
            dyb[j * L:(j + 1) * L, :] = rdy[:, :, j * D:(j + 1) * D].reshape(L, D)
        for j in range(lo, hi):
            jr = slice(j * L, (j + 1) * L)
            g = jnp.zeros((L, L), f32)
            for n in range(D // L):
                cols = slice(n * L, (n + 1) * L)
                v = dyb[jr, cols].astype(f32)
                dhb[0, jr, cols] = (pe_scr[jr, :] * v).astype(bf16)
                g = g + v * hb[jr, cols].astype(f32)
            wide = jnp.where(lane == 2 * j + odd, jnp.sum(g, axis=1, keepdims=True), wide)
        sw_dh.append(swap(dhb.at[0, rows], dhb.at[1, rows], 2 + b))
        sw_dh[b].start()
        if b == 1:
            gs[...] = wide.reshape(N, 2, L)
            send_all(*g_io)
        for s in range(2):
            for n in range(H // FT):
                cols = slice(n * FT, (n + 1) * FT)
                v = dot(dhb[0, rows, :], wout[pl.ds(halves[s] + n * FT, FT), :], 1, 1)
                da[s, rows, cols] = jnp.where(act[s, rows, cols] > 0, v, 0.0).astype(bf16)
            if s == 0:
                sw_da.append(swap(da.at[0, rows], da.at[2, rows], 4 + b))
                sw_da[b].start()
        for n in range(D // DT):
            dr = slice(n * DT, (n + 1) * DT)
            v = (dot(da[0, rows, :], win[dr, pl.ds(ot_h, H)], 1, 1) + dot(da[1, rows, :], win[dr, pl.ds(my_h, H)], 1, 1)).astype(bf16)
            for j in range(lo, hi):
                sx[:, :, j * D + n * DT:j * D + (n + 1) * DT] = v[(j - lo) * L:(j - lo + 1) * L, :].reshape(N, 2, DT)
        send_all(*bk_io[b])

    sw_x.wait()
    sw_act.wait()
    sw_dh[0].wait()
    sw_dh[1].wait()
    col = jnp.zeros((8, D), f32)
    for n in range(H // FT):
        cols = slice(n * FT, (n + 1) * FT)
        v = dot(act[1:3, :, cols].reshape(2 * R, FT), dhb[...].reshape(2 * R, D), 0, 0)
        gout[cols, :] = v
        sq = v * v
        part = sum(sq[:, m * L:(m + 1) * L] for m in range(D // L))
        rsum = jnp.sum(tr(part), axis=0, keepdims=True)
        hs_s[0, :, cols] = DECAY * rout_ref[:, pl.ds(my_h + n * FT, FT)] + (1.0 - DECAY) * (rsum * (1.0 / D) + 1e-30)
        col = col + jnp.sum(sq.reshape(FT // 8, 8, D), axis=0)
    st_s[0] = jnp.broadcast_to(jnp.sum(col, axis=0, keepdims=True), (8, D))
    sw_c = swap(st_s.at[0], st_r.at[0], 6)
    sw_c.start()

    done_all(*g_io).wait_recv()
    gr[pl.ds(me, 1)] = gs[pl.ds(me, 1)]
    gsum = gr[:, 0, :] + gr[:, 1, :]
    onehot = oh_tok[...]
    ohb = onehot[:, :N].astype(bf16)
    ghi, gmid, glo = split3(gsum)
    gt = (dot(ohb, glo, 1, 0) + dot(ohb, gmid, 1, 0)) + dot(ohb, ghi, 1, 0)
    slot_col = tr(jnp.broadcast_to(slot_ref[...].astype(f32), (L, T)))
    gtok = jnp.sum(jnp.where(lane_t.astype(f32) == slot_col, gt, 0.0), axis=1, keepdims=True)
    frac = jnp.sum(onehot, axis=0, keepdims=True) * (1.0 / T)
    prob = p_tok[...]
    dprob = onehot * gtok + (AUX * N / T) * frac
    dlog = prob * (dprob - jnp.sum(prob * dprob, axis=1, keepdims=True))
    dhi, dmid, dlo = split3(dlog)
    xs = xv[...]
    dwr = (dot(dlo, xs, 0, 0) + dot(dmid, xs, 0, 0)) + dot(dhi, xs, 0, 0)
    rs_s[...] = dwr[:N].reshape(N, 1, D)
    send_all(*rs_io)

    sw_da[0].wait()
    sw_da[1].wait()

    def gin_tile(n, racc):
        cols = slice(n * FT, (n + 1) * FT)
        v = dot(xb[...].reshape(2 * R, D), da[1:3, :, cols].reshape(2 * R, FT), 0, 0)
        gin[:, cols] = v
        sq = v * v
        csum = jnp.sum(sq, axis=0, keepdims=True)
        hs_s[1, :, cols] = DECAY * cin_ref[:, pl.ds(my_h + n * FT, FT)] + (1.0 - DECAY) * (csum * (1.0 / D) + 1e-30)
        return racc + sum(sq[:, m * L:(m + 1) * L] for m in range(FT // L))

    racc = gin_tile(0, jnp.zeros((D, L), f32))

    sw_c.wait()
    ctot = st_s[0, 0:1, :] + st_r[0, 0:1, :]
    cout_n = DECAY * cout_ref[...] + (1.0 - DECAY) * (ctot * (1.0 / F) + 1e-30)
    cout_new[...] = cout_n
    mean_r = DECAY * mean1(rout_ref[...]) + (1.0 - DECAY) * (mean1(ctot) * (1.0 / F) + 1e-30)
    a_out = lax.rsqrt(hs_s[0] / mean_r)
    b_out = lax.rsqrt(cout_n)

    def scale(ref, a, b, rows, cols):
        usq = jnp.zeros((8, L), f32)
        for n in range(rows // L):
            sc = tr(jnp.broadcast_to(a[:, n * L:(n + 1) * L], (L, L)))
            for m in range(cols // L):
                lanes = slice(m * L, (m + 1) * L)
                u = ref[n * L:(n + 1) * L, lanes] * sc * b[:, lanes]
                ref[n * L:(n + 1) * L, lanes] = u
                usq = usq + jnp.sum((u * u).reshape(L // 8, 8, L), axis=0)
        return total(usq)

    st_s[2, :, :L] = jnp.broadcast_to(scale(gout, a_out, b_out, H, D), (8, L))
    sw_uo = swap(st_s.at[2, :, pl.ds(0, L)], st_r.at[2, :, pl.ds(0, L)], 8)
    sw_uo.start()
    racc = gin_tile(1, racc)
    sw_uo.wait()
    uso = st_s[2, 0:1, 0:1] + st_r[2, 0:1, 0:1]
    k_out = LR * jnp.maximum(1e-3, wout_rms) / jnp.maximum(1.0, jnp.sqrt(uso * (1.0 / (D * F))))
    for n in range(H // L):
        rows = pl.ds(my_h + n * L, L)
        wout_new[0, rows, :] = (wout[rows, :].astype(f32) - k_out * gout[n * L:(n + 1) * L, :]).astype(bf16)
    out_half = wout_new.at[0, pl.ds(my_h, H), :]
    sw_wo = swap(out_half, out_half, 9)
    sw_wo.start()
    done_all(*rs_io).wait_recv()
    rs_r[pl.ds(me, 1)] = rs_s[pl.ds(me, 1)]
    st_s[3] = jnp.broadcast_to(jnp.sum(rs_r[...], axis=0), (8, D))
    sw_r = swap(st_s.at[3], st_r.at[3], 10)
    sw_r.start()
    racc = gin_tile(2, racc)
    st_s[1] = jnp.broadcast_to(jnp.sum(tr(racc), axis=0, keepdims=True), (8, D))
    sw_ri = swap(st_s.at[1], st_r.at[1], 7)
    sw_ri.start()
    sw_hs = swap(hs_s, hs_r, 11)
    sw_hs.start()
    sw_r.wait()
    ag_s[...] = st_s[3, 0:1, :] + st_r[3, 0:1, :]
    send_all(lambda p: ag_s, lambda p: ag_r.at[p], ags, agr)
    w6 = jnp.concatenate([wr3[:L], wr3[L:2 * L], wr3[:L], wr3[L:2 * L], wr3[2 * L:], wr3[:L]], axis=0)
    d6 = jnp.concatenate([dhi, dhi, dmid, dmid, dhi, dlo], axis=1)
    dxr = dot(d6, w6, 1, 0)

    sw_ri.wait()
    rtot = st_s[1, 0:1, :] + st_r[1, 0:1, :]
    rin_n = DECAY * rin_ref[...] + (1.0 - DECAY) * (rtot * (1.0 / F) + 1e-30)
    rin_new[...] = rin_n
    a_in = lax.rsqrt(rin_n / mean1(rin_n))
    b_in = lax.rsqrt(hs_s[1])
    st_s[2, :, L:2 * L] = jnp.broadcast_to(scale(gin, a_in, b_in, D, H), (8, L))
    sw_ui = swap(st_s.at[2, :, pl.ds(L, L)], st_r.at[2, :, pl.ds(L, L)], 12)
    sw_ui.start()

    for b, (lo, hi) in enumerate(BLOCKS):
        done_all(*bk_io[b]).wait()
        back[pl.ds(me, 1), :, lo * D:hi * D] = sx[pl.ds(me, 1), :, lo * D:hi * D]
    for j in range(J):
        dyb[j * L:(j + 1) * L, :] = back[:, :, j * D:(j + 1) * D].reshape(L, D)
    dx_ref[...] = (dot(t_oh[...], dyb[...], 1, 0) + dxr).astype(bf16)

    sw_ui.wait()
    usi = st_s[2, 0:1, L:L + 1] + st_r[2, 0:1, L:L + 1]
    k_in = LR * jnp.maximum(1e-3, win_rms) / jnp.maximum(1.0, jnp.sqrt(usi * (1.0 / (D * F))))
    sw_wi = []
    for n in range(D // L):
        rows = slice(n * L, (n + 1) * L)
        win_new[0, rows, pl.ds(my_h, H)] = (win[rows, pl.ds(my_h, H)].astype(f32) - k_in * gin[rows, :]).astype(bf16)
        if n % 2 == 1:
            part = win_new.at[0, (n - 1) * L:(n + 1) * L, pl.ds(my_h, H)]
            sw_wi.append(swap(part, part, 13 + n // 2))
            sw_wi[-1].start()

    done_all(lambda p: ag_r.at[p], lambda p: ag_r.at[p], ags, agr).wait()
    ag_r[me] = ag_s[...]
    grt = ag_r[...].reshape(N, D)
    sq = grt * grt
    rr_n = DECAY * rr_ref[...] + (1.0 - DECAY) * (jnp.sum(sq, axis=0, keepdims=True) * (1.0 / N) + 1e-30)
    rr_new[...] = rr_n
    cmean = jnp.sum(sq, axis=1, keepdims=True) * (1.0 / D) + 1e-30
    cr_col = tr(jnp.broadcast_to(jnp.concatenate([cr_ref[...], jnp.ones((1, L - N), f32)], axis=1), (L, L)))[:N, 0:1]
    cr_n = DECAY * cr_col + (1.0 - DECAY) * cmean
    cr_new[...] = tr(jnp.broadcast_to(jnp.concatenate([cr_n, jnp.ones((L - N, 1), f32)], axis=0), (L, L)))[0:1, :N]
    u = grt * lax.rsqrt(rr_n / mean1(rr_n)) * lax.rsqrt(cr_n)
    urms = jnp.sqrt(total(u * u) * (1.0 / (D * N)))
    k_r = LR * jnp.maximum(1e-3, wr_rms) / jnp.maximum(1.0, urms)
    wrt_new[...] = wrt_ref[...] - k_r * u

    done_all(*dy_io[1]).wait_send()
    done_all(*g_io).wait_send()
    done_all(*rs_io).wait_send()
    sw_hs.wait()
    for ref, n in ((rout_new, 0), (cin_new, 1)):
        ref[:, pl.ds(my_h, H)] = hs_s[n]
        ref[:, pl.ds(ot_h, H)] = hs_r[n]
    sw_wo.wait()
    for cp in sw_wi:
        cp.wait()


def finish(*refs):
    n = len(refs) // 2
    sems = refs[-1]
    copies = [pltpu.make_async_copy(refs[k], refs[n + k], sems.at[k]) for k in range(n)]
    for copy in copies:
        copy.start()
    for copy in copies:
        copy.wait()


def solution(mesh):
    tok = P(("dp", "ep"))
    row = P(("dp", "ep"), None)
    exp = P("ep")
    full = P()
    dma = pltpu.SemaphoreType.DMA
    vm = pl.BlockSpec(memory_space=VMEM)
    hb = pl.BlockSpec(memory_space=pl.ANY)

    def local_step(x, eid, slot, dy, wr, win, wout, rin, cin, rout, cout, rr, cr):
        shapes = (((1, D, F), bf16), ((1, F, D), bf16), ((N, D), f32), ((1, D), f32), ((1, F), f32), ((1, F), f32),
                  ((1, D), f32), ((1, D), f32), ((1, N), f32), ((T, D), bf16))
        outs = pl.pallas_call(
            kernel,
            out_shape=tuple(VMEM(*s) for s in shapes),
            in_specs=[hb, hb, vm, vm, vm, hb, hb] + [vm] * 6,
            out_specs=(vm,) * 10,
            scratch_shapes=[
                VMEM((D, F), bf16), VMEM((F, D), bf16), VMEM((T, D), bf16), VMEM((T, D), bf16),
                VMEM((N, 2, J * D), bf16), VMEM((N, 2, J * D), bf16), VMEM((N, 2, J * D), bf16), VMEM((N, 2, J * D), bf16),
                VMEM((2, R, D), bf16), VMEM((R, D), bf16), VMEM((R, D), bf16), VMEM((2, R, D), bf16),
                VMEM((3, R, H), bf16), VMEM((3, R, H), bf16),
                VMEM((H, D), f32), VMEM((D, H), f32),
                VMEM((3 * L, D), bf16), VMEM((T, L), f32), VMEM((T, L), f32), VMEM((T, R), bf16),
                VMEM((R, L), f32), VMEM((N, 2, L), f32), VMEM((N, 2, L), f32),
                VMEM((N, 1, D), f32), VMEM((N, 1, D), f32), VMEM((1, D), f32), VMEM((N, 1, D), f32), VMEM((N, 2, J * D), bf16),
                VMEM((4, 8, D), f32), VMEM((4, 8, D), f32), VMEM((2, 1, H), f32), VMEM((2, 1, H), f32),
                dma((4,)),
                dma, dma, dma((2,)), dma((2,)), dma, dma, dma((2,)), dma((2,)), dma, dma, dma, dma, dma((16,)), dma((16,)),
            ],
            compiler_params=pltpu.CompilerParams(collective_id=1, has_side_effects=True, vmem_limit_bytes=52 * 2**20),
            name="expert_step",
        )(x, dy, eid.reshape(1, T), slot.reshape(1, T), wr.T, win, wout, rin, cin, rout, cout, rr.reshape(1, D), cr.reshape(1, N))
        outs = pl.pallas_call(
            finish,
            out_shape=tuple(jax.ShapeDtypeStruct(*s) for s in shapes),
            in_specs=[vm] * 10,
            out_specs=(hb,) * 10,
            scratch_shapes=[dma((10,))],
            compiler_params=pltpu.CompilerParams(vmem_limit_bytes=2**20),
            name="write_out",
        )(*outs)
        return outs[:2] + (outs[2].T,) + outs[3:7] + (outs[7].reshape(D), outs[8].reshape(N), outs[9])

    in_specs = (row, tok, tok, row, full, exp, exp, exp, exp, exp, exp, full, full)
    out_specs = (exp, exp, full, exp, exp, exp, exp, full, full, row)
    return jax.shard_map(local_step, mesh=mesh, in_specs=in_specs, out_specs=out_specs, check_vma=False)
```

time: 393 us -> 81.9 us (0.21)
  waiting for transfers between devices: 155 us -> 0 us
  Pallas kernels: 0 us -> 79.2 us
  other arithmetic: 74.8 us -> 0.61 us
  matrix products: 40.7 us -> 0 us
  blocking collectives: 38.7 us -> 0 us
  local copies, waits for them, and re-layouts: 38.9 us -> 1.27 us
  between operations: 21.1 us -> 0.66 us
  starting transfers between devices: 20 us -> 0 us
    psum x2 -> x0, waiting for transfers between devices: 103 us -> none  [the longest x1 94.4 us: local_step(): lax.psum(jnp.einsum('td,te->de', x_wide, grad_logits, precision=PRECISE),...]
    pallas_call x0 -> x2, Pallas kernels: none -> 79.2 us  [the longest x1 75.2 us: local_step(): pl.pallas_call(kernel, out_shape=tuple((VMEM(*s) for s in shapes)), in_sp...]
    all_to_all x3 -> x0, waiting for transfers between devices: 52.7 us -> none  [the longest x2 27.8 us: to_tokens(): lax.all_to_all(expert_rows.reshape(1, experts_local, ep_size * capacity,...]
    dot_general x9 -> x0, matrix products: 40.7 us -> none  [the longest x1 7.22 us: local_step(): jnp.einsum('erd,efd->erf', recv_gh, w_out, preferred_element_type=jnp.flo...]
    all_to_all x1 -> x0, blocking collectives: 38.7 us -> none  [to_experts(): recv_buf = lax.all_to_all(send_buf, 'ep', 0, 2, tiled=True)]
    reduce_sum x14 -> x0, other arithmetic: 37.1 us -> none  [the longest x3 13.9 us: optimizer_step(): upd_rms = jnp.sqrt(jnp.mean(update * update, axis=(-2, -1), keepdims=True))]
    all_to_all x3 -> x0, starting transfers between devices: 19.9 us -> none  [the longest x2 12.4 us: to_tokens(): lax.all_to_all(expert_rows.reshape(1, experts_local, ep_size * capacity,...]
    unnamed x77 -> x0, local copies, waits for them, and re-layouts: 18.4 us -> none
  transfers between devices with their start and end apart: 5 -> 0, of which waited for: 5 -> 0; matrix products, arithmetic and copies ran while one was open for 17% -> 0% of each run, Pallas kernels for 0% -> 0%
where the time goes in v1:
time: 81.9 us; the launch traced here: 81.7 us
  Pallas kernels  79.2 us (97%)
  local copies, waits for them, and re-layouts  1.27 us (2%)
    pallas_call x1, Pallas kernels, local_step(): pl.pallas_call(kernel, out_shape=tuple((VMEM(*s) for s in shapes)), in_sp...  75.2 us
    pallas_call x1, Pallas kernels, local_step(): pl.pallas_call(finish, out_shape=tuple((jax.ShapeDtypeStruct(*s) for s in...  4.03 us

profile of v1, /device:TPU:1, one launch (start us, length us, event | category | flops | bytes accessed | tf_op | source)
XLA Modules:
  0.0 81.7 jit_solution(2445830320606905595)
XLA Ops:
  0.6 1.3 %reshape.40.rr_ref = f32[1,768]{1,0:T(1,128)} reshape(f32[768]{0:T(1024)} %param.24) | data formatting | bytes 6144 | tf_op jit(solution)/shard_map/reshape | solution.py:428
  1.9 75.2 %expert_step.1 = (bf16[1,768,3072]{2,1,0:T(8,128)(2,1)S(1)}, bf16[1,3072,768]{2,1,0:T(8,128)(2,1)S(1)}, f32[64,768]{1,0:T(8,128)S(1)}, f32[1,768]{1,0:T(1,128)S(...) custom-call(bf16[512,768]{1,0:T(8,128)(2,1)} %x_hbm.1, ...), custom_call_target="tpu_custom_call" | custom-call | tf_op jit(solution)/shard_map/expert_step/pallas_call | solution.py:408
  77.1 4.0 %write_out.1 = (bf16[1,768,3072]{2,1,0:T(8,128)(2,1)}, bf16[1,3072,768]{2,1,0:T(8,128)(2,1)}, f32[64,768]{1,0:T(8,128)}, f32[1,768]{1,0:T(1,128)}, f32[1,3072]{1...) custom-call(bf16[1,768,3072]{2,1,0:T(8,128)(2,1)S(1)} %get-tuple-ele, ...), custom_call_target="tpu_custom_call" | custom-call | tf_op jit(solution)/shard_map/write_out/pallas_call | solution.py:429
  81.1 0.6 reduce
